TPU v7x, 32 devices: a whole 2x2x4 slice. The times are simulated.
32 devices in a mesh: batch: 4 (over x, core), lat: 8 (over z, y).
Axes of the slice: x: 2, y: 2, z: 4, core: 2. Of those that a mesh axis runs over, the one named last changes fastest.
Arguments:
- predicted: bfloat16 [4, 73, 192, 1440], P('batch', None, 'lat'), may hold values from -64 to 64
- target: bfloat16 [4, 73, 192, 1440], P('batch', None, 'lat'), may hold values from -128 to 128
- legendre_basis: bfloat16 [192, 96, 720], P(None, ('batch', 'lat')), may hold values from -1 to 1
Outputs:
- spectra: float32 [2, 73, 720], replicated
- channel_loss: float32 [73], replicated
All inputs are finite; a program needn't handle non-finite values.
Results may differ from a plain program's by a relative error of at most 0.0003.
Values may be sent and summed in bfloat16 or wider, within the bound.
No kernel may reach another device: no remote copies, remote signals or barrier semaphores. Data moves between devices by JAX's collectives and lax.ppermute only.
A program may use at most 128 MiB of HBM per device.

v0:
```python
import math
import jax
import jax.numpy as jnp
from jax import lax
from jax.sharding import PartitionSpec as P


def fourier_table(lon_count, order_count):
    lon_ids = jnp.arange(lon_count, dtype=jnp.int32)
    order_ids = jnp.arange(order_count, dtype=jnp.int32)
    product_ids = lon_ids[:, None] * order_ids[None, :] % lon_count
    angles = 2.0 * math.pi / lon_count * product_ids.astype(jnp.float32)
    inv_root = 1.0 / math.sqrt(lon_count)
    return jnp.stack([jnp.cos(angles) * inv_root, -jnp.sin(angles) * inv_root], axis=1).astype(
        jnp.bfloat16
    )


def band_energy(fourier, basis_block, orders):
    coefficients = jnp.einsum(
        "fpmbcn,nml->fpmbcl", fourier, basis_block, preferred_element_type=jnp.float32
    )
    squares = jnp.sum(coefficients * coefficients, axis=1)
    weights = jnp.where(orders == 0, 1.0, 2.0).astype(jnp.float32)
    return jnp.sum(squares * weights[None, :, None, None, None], axis=(1, 2))


def body(predicted, target, legendre_basis):
    groups = lax.axis_size("batch")
    band_count = lax.axis_size("lat")
    per_dev = legendre_basis.shape[1]
    order_count = per_dev * groups * band_count
    dft_table = fourier_table(predicted.shape[3], order_count)
    band_id = lax.axis_index("lat")

    def transform(field_in):
        return jnp.einsum(
            "bcnk,kpm->pmbcn", field_in, dft_table, preferred_element_type=jnp.float32
        ).astype(jnp.bfloat16)

    fourier = jnp.stack([transform(predicted), transform(target)], axis=0)
    members = fourier.shape[3]
    channels = fourier.shape[4]
    lat_rows = fourier.shape[5]
    fourier = fourier.reshape(2, 2, groups, band_count, per_dev, members, channels, lat_rows)
    arrived = lax.all_to_all(fourier, "lat", split_axis=3, concat_axis=7, tiled=True)
    arrived = arrived.reshape(
        2, 2, groups * per_dev, arrived.shape[5], arrived.shape[6], arrived.shape[7]
    )
    basis_block = lax.all_gather(legendre_basis, "batch", axis=1, tiled=True)
    taken = basis_block.shape[1]
    gathered_ids = jnp.arange(taken, dtype=jnp.int32)
    orders = (
        gathered_ids // per_dev * band_count * per_dev + band_id * per_dev + gathered_ids % per_dev
    )
    partial_value = band_energy(arrived, basis_block, orders)
    energy = lax.psum(partial_value, "lat")
    energy = lax.psum(energy, "batch")
    spectra = energy / (predicted.shape[0] * groups * order_count)
    log_spectra = jnp.log(spectra + 1e-06)
    channel_loss = jnp.mean((log_spectra[0] - log_spectra[1]) ** 2, axis=1)
    return (spectra, channel_loss)


def solution(mesh):
    placed = (
        P("batch", None, "lat", None),
        P("batch", None, "lat", None),
        P(None, ("batch", "lat"), None),
    )
    return jax.shard_map(body, mesh=mesh, in_specs=placed, out_specs=(P(), P()), check_vma=False)
```

profile of v0, /device:TPU:0, one launch (start us, length us, event | category | flops | bytes accessed | tf_op | source)
XLA Modules:
  0.0 212.2 jit_solution(11625327290755649896)
XLA Ops:
  7.2 0.0 all-gather.2.cloned.1.call-start
  7.2 0.7 all-gather.2.cloned.1.call-update
  7.9 2.6 %multiply_convert_fusion = (bf16[1440,1,96]{0,2,1:T(8,128)(2,1)S(1)}, bf16[1440,1,96]{0,2,1:T(8,128)(2,1)S(1)}) fusion(), kind=kLoop, calls=%fused_computation.17 | loop fusion | flops 1935360 | bytes 552960 | tf_op jit(solution)/shard_map/convert.1
  10.5 0.0 copy-start
  10.5 0.0 copy-start.1
  10.5 0.7 copy-done
  11.2 0.1 copy-done.1
  11.3 4.8 %fusion.8 = bf16[2,96,73,24]{1,2,3,0:T(8,128)(2,1)S(1)} fusion(bf16[73,24,1440]{2,1,0:T(8,128)(2,1)} %bitcast.33, bf16[1440,1,96]{0,2,1:T(8,128)(2,1)S(1)} %get-tuple-element.4, bf16[1440,1,96]{0,2,1:T(8,128)(2,1)S(1)} %get-tuple-element.5), kind=kOutput, calls=%fused_computation.11 | convolution fusion | flops 970228224 | bytes 6271488 | tf_op jit(solution)/shard_map/bcnk,kpm->pmbcn/dot_general | solution.py:37
  16.1 0.9 copy.29
  17.0 5.5 %fusion.11 = bf16[2,96,73,24]{1,2,3,0:T(8,128)(2,1)S(1)} fusion(bf16[73,24,1440]{2,1,0:T(8,128)(2,1)} %bitcast.34, bf16[1440,1,96]{0,2,1:T(8,128)(2,1)} %copy-done, bf16[1440,1,96]{0,2,1:T(8,128)(2,1)} %copy-done.1), kind=kOutput, calls=%fused_computation.12 | convolution fusion | flops 970228224 | bytes 6271488 | tf_op jit(solution)/shard_map/bcnk,kpm->pmbcn/dot_general | solution.py:37
  22.5 0.9 copy.31
  23.3 0.5 pad_maximum_fusion
  23.9 2.0 copy.32
  25.9 7.5 %all-to-all-start = ((bf16[2,2,4,8,3,1,73,24]{6,7,4,2,1,5,0,3:T(8,128)(2,1)}), bf16[2,2,4,8,3,1,73,24]{6,7,4,2,1,5,0,3:T(8,128)(2,1)S(1)}, u32[]{:S(2)}, u32[]{:S(2)}) async-start(bf16[2,2,4,8,3,1,73,24]{6,7,4,2,1,5,0,3:T(8,128)(2,1)} %copy.32), calls=%async_computation | async-start | bytes 4718592 | tf_op jit(solution)/shard_map/all_to_all | solution.py:46
  33.5 0.0 all-reduce.3.cloned.1.call-start
  33.5 53.6 %all-to-all-done = bf16[2,2,4,8,3,1,73,24]{6,7,4,2,1,5,0,3:T(8,128)(2,1)S(1)} async-done(((bf16[2,2,4,8,3,1,73,24]{6,7,4,2,1,5,0,3:T(8,128)(2,1)}), bf16[2,2,4,8,3,1,73,24]{6,7,4,2,1,5,0,3:T(8,128)(2,1)S(1)}, u32[]{:S(2)}, u32[]{:S(2)}) %all-to-all-start) | async-done | bytes 1345568 | tf_op jit(solution)/shard_map/all_to_all | solution.py:46
  87.1 2.1 copy.33
  89.2 0.0 all-gather.2.cloned.1.call-done
  89.2 5.1 %multiply_reduce_fusion = f32[12,2,73,720]{3,2,1,0:T(8,128)S(1)} fusion(bf16[192,12,720]{2,0,1:T(8,128)(2,1)} %all-gather.2.cloned.1.call-done, bf16[2,2,12,73,192]{3,4,2,1,0:T(8,128)(2,1)} %bitcast.30), kind=kOutput, calls=%fused_computation | convolution fusion | flops 972570240 | bytes 9709056 | tf_op jit(solution)/shard_map/fpmbcn,nml->fpmbcl/dot_general | solution.py:20
  94.3 0.6 multiply_reduce_fusion.1
  94.9 1.1 copy.40
  96.0 0.0 all-reduce.3.cloned.1.call-update
  96.1 0.0 all-reduce.5.cloned.1.call-start
  96.1 71.4 %all-reduce.3.cloned.1.call-done = f32[2,73,720]{2,0,1:T(2,128)} async-done(((f32[2,73,720]{2,0,1:T(2,128)}), f32[2,73,720]{2,0,1:T(2,128)}) %all-reduce.3.cloned.1.call-update) | async-done | bytes 420496 | tf_op jit(solution)/shard_map/psum | solution.py:57
  167.5 0.0 all-reduce.5.cloned.1.call-update
  167.6 34.7 %all-reduce.5.cloned.1.call-done = f32[2,73,720]{2,0,1:T(2,128)} async-done(((f32[2,73,720]{2,0,1:T(2,128)}), f32[2,73,720]{2,0,1:T(2,128)}) %all-reduce.5.cloned.1.call-update) | async-done | bytes 420496 | tf_op jit(solution)/shard_map/psum | solution.py:58
  202.2 2.2 %add_log_fusion = (f32[2,73,720]{2,0,1:T(2,128)S(1)}, f32[2,73,720]{2,0,1:T(2,128)}) fusion(f32[2,73,720]{2,0,1:T(2,128)} %all-reduce.5.cloned.1.call-done), kind=kLoop, calls=%fused_computation.23 | loop fusion | flops 210240 | bytes 1261440 | tf_op jit(solution)/shard_map/log | solution.py:60
  204.5 0.6 fusion.20
  205.1 0.5 broadcast_multiply_fusion.1
  (1 shorter events, 0.0 us)
Async XLA Ops:
  7.2 82.1 %all-gather.2.cloned.1.call-start = ((), (), s32[]{:S(2)}) async-start(), calls=%async_computation.1 | async-start | bytes 4423680 | tf_op jit(solution)/shard_map/all_gather | solution.py:50
  10.5 0.7 copy-start
  10.5 0.8 copy-start.1
  25.9 61.2 %all-to-all-start = ((bf16[2,2,4,8,3,1,73,24]{6,7,4,2,1,5,0,3:T(8,128)(2,1)}), bf16[2,2,4,8,3,1,73,24]{6,7,4,2,1,5,0,3:T(8,128)(2,1)S(1)}, u32[]{:S(2)}, u32[]{:S(2)}) async-start(bf16[2,2,4,8,3,1,73,24]{6,7,4,2,1,5,0,3:T(8,128)(2,1)} %copy.32), calls=%async_computation | async-start | bytes 4718592 | tf_op jit(solution)/shard_map/all_to_all | solution.py:46
  33.5 134.1 %all-reduce.3.cloned.1.call-start = ((), (), s32[]{:S(2)}) async-start(), calls=%async_computation.2 | async-start | bytes 897024 | tf_op jit(solution)/shard_map/psum | solution.py:57
  96.1 106.2 %all-reduce.5.cloned.1.call-start = ((), (), s32[]{:S(2)}) async-start(), calls=%async_computation.3 | async-start | bytes 897024 | tf_op jit(solution)/shard_map/psum | solution.py:58
Sparse Core Ops, SparseCore 0:
  9.5 33.4 all-gather.1
  96.2 71.2 all-reduce.2
  169.9 32.2 all-reduce.4
where the time goes:
time: 212 us
  waiting for transfers between devices  160 us (75%)
  matrix products  15.4 us (7%)
  between operations  13.8 us (7%)
  local copies, waits for them, and re-layouts  7.77 us (4%)
  starting transfers between devices  7.66 us (4%)
  other arithmetic  7.07 us (3%)
    psum x1, waiting for transfers between devices, body(): energy = lax.psum(partial_value, 'lat')  71.4 us
    all_to_all x1, waiting for transfers between devices, body(): lax.all_to_all(fourier, 'lat', split_axis=3, concat_axis=7, tiled=True)  53.6 us
    psum x1, waiting for transfers between devices, body(): energy = lax.psum(energy, 'batch')  34.7 us
    dot_general x2, matrix products, transform(): jnp.einsum('bcnk,kpm->pmbcn', field_in, dft_table, preferred_element_type...  10.3 us
    all_to_all x1, starting transfers between devices, body(): lax.all_to_all(fourier, 'lat', split_axis=3, concat_axis=7, tiled=True)  7.55 us
    dot_general x1, matrix products, band_energy(): jnp.einsum('fpmbcn,nml->fpmbcl', fourier, basis_block, preferred_element_...  5.1 us
  transfers between devices with their start and end apart: 4, of which 3 were waited for; matrix products, arithmetic and copies ran while one was open for 9% of the time, Pallas kernels for 0%

commit v1 on v0

--- a/solution.py
+++ b/solution.py
@@ -3,6 +3,11 @@
 import jax.numpy as jnp
 from jax import lax
 from jax.sharding import PartitionSpec as P
+
+
+def gather_and_add(x, mesh_axis):
+    parts = lax.all_gather(x, mesh_axis)
+    return jnp.sum(parts, axis=0)
 
 
 def fourier_table(lon_count, order_count):
@@ -55,7 +60,7 @@
     )
     partial_value = band_energy(arrived, basis_block, orders)
     energy = lax.psum(partial_value, "lat")
-    energy = lax.psum(energy, "batch")
+    energy = gather_and_add(energy, "batch")
     spectra = energy / (predicted.shape[0] * groups * order_count)
     log_spectra = jnp.log(spectra + 1e-06)
     channel_loss = jnp.mean((log_spectra[0] - log_spectra[1]) ** 2, axis=1)

time: 212 us -> 201 us (0.948)
  waiting for transfers between devices: 160 us -> 148 us
    psum x1 -> x0, waiting for transfers between devices: 34.7 us -> none  [body(): energy = lax.psum(energy, 'batch')]
    all_gather x0 -> x1, waiting for transfers between devices: none -> 21.8 us  [gather_and_add(): parts = lax.all_gather(x, mesh_axis)]
    reduce_sum x0 -> x1, other arithmetic: none -> 2.36 us  [gather_and_add(): return jnp.sum(parts, axis=0)]
  transfers between devices with their start and end apart: 4 -> 4, of which waited for: 3 -> 3; matrix products, arithmetic and copies ran while one was open for 9% -> 10% of each run, Pallas kernels for 0% -> 0%
where the time goes in v1:
time: 201 us
  waiting for transfers between devices  148 us (74%)
  matrix products  15.4 us (8%)
  between operations  13.8 us (7%)
  other arithmetic  8.42 us (4%)
  local copies, waits for them, and re-layouts  7.77 us (4%)
  starting transfers between devices  7.66 us (4%)
    psum x1, waiting for transfers between devices, body(): energy = lax.psum(partial_value, 'lat')  71.4 us
    all_to_all x1, waiting for transfers between devices, body(): lax.all_to_all(fourier, 'lat', split_axis=3, concat_axis=7, tiled=True)  53.6 us
    all_gather x1, waiting for transfers between devices, gather_and_add(): parts = lax.all_gather(x, mesh_axis)  21.8 us
    dot_general x2, matrix products, transform(): jnp.einsum('bcnk,kpm->pmbcn', field_in, dft_table, preferred_element_type...  10.3 us
    all_to_all x1, starting transfers between devices, body(): lax.all_to_all(fourier, 'lat', split_axis=3, concat_axis=7, tiled=True)  7.55 us
    dot_general x1, matrix products, band_energy(): jnp.einsum('fpmbcn,nml->fpmbcl', fourier, basis_block, preferred_element_...  5.1 us
  transfers between devices with their start and end apart: 4, of which 3 were waited for; matrix products, arithmetic and copies ran while one was open for 10% of the time, Pallas kernels for 0%

profile of v1, /device:TPU:0, one launch (start us, length us, event | category | flops | bytes accessed | tf_op | source)
XLA Modules:
  0.0 200.7 jit_solution(17926567921007779769)
XLA Ops:
  7.2 0.0 all-gather.3.cloned.1.call-start
  7.2 0.7 all-gather.3.cloned.1.call-update
  7.9 2.6 %multiply_convert_fusion = (bf16[1440,1,96]{0,2,1:T(8,128)(2,1)S(1)}, bf16[1440,1,96]{0,2,1:T(8,128)(2,1)S(1)}) fusion(), kind=kLoop, calls=%fused_computation.17 | loop fusion | flops 1935360 | bytes 552960 | tf_op jit(solution)/shard_map/convert.1
  10.5 0.0 copy-start
  10.5 0.0 copy-start.1
  10.5 0.7 copy-done
  11.2 0.1 copy-done.1
  11.3 4.8 %fusion.8 = bf16[2,96,73,24]{1,2,3,0:T(8,128)(2,1)S(1)} fusion(bf16[73,24,1440]{2,1,0:T(8,128)(2,1)} %bitcast.37, bf16[1440,1,96]{0,2,1:T(8,128)(2,1)S(1)} %get-tuple-element.4, bf16[1440,1,96]{0,2,1:T(8,128)(2,1)S(1)} %get-tuple-element.5), kind=kOutput, calls=%fused_computation.11 | convolution fusion | flops 970228224 | bytes 6271488 | tf_op jit(solution)/shard_map/bcnk,kpm->pmbcn/dot_general | solution.py:42
  16.1 0.9 copy.29
  17.0 5.5 %fusion.11 = bf16[2,96,73,24]{1,2,3,0:T(8,128)(2,1)S(1)} fusion(bf16[73,24,1440]{2,1,0:T(8,128)(2,1)} %bitcast.38, bf16[1440,1,96]{0,2,1:T(8,128)(2,1)} %copy-done, bf16[1440,1,96]{0,2,1:T(8,128)(2,1)} %copy-done.1), kind=kOutput, calls=%fused_computation.12 | convolution fusion | flops 970228224 | bytes 6271488 | tf_op jit(solution)/shard_map/bcnk,kpm->pmbcn/dot_general | solution.py:42
  22.5 0.9 copy.31
  23.3 0.5 pad_maximum_fusion
  23.9 2.0 %copy.32 = bf16[2,2,4,8,3,1,73,24]{6,7,4,2,1,5,0,3:T(8,128)(2,1)} copy(bf16[2,2,4,8,3,1,73,24]{6,7,4,3,2,1,5,0:T(8,128)(2,1)S(1)} %pad_maximum_fusion) | data formatting | bytes 2691072 | tf_op jit(solution)/shard_map/stack | solution.py:46
  25.9 7.5 %all-to-all-start = ((bf16[2,2,4,8,3,1,73,24]{6,7,4,2,1,5,0,3:T(8,128)(2,1)}), bf16[2,2,4,8,3,1,73,24]{6,7,4,2,1,5,0,3:T(8,128)(2,1)S(1)}, u32[]{:S(2)}, u32[]{:S(2)}) async-start(bf16[2,2,4,8,3,1,73,24]{6,7,4,2,1,5,0,3:T(8,128)(2,1)} %copy.32), calls=%async_computation | async-start | bytes 4718592 | tf_op jit(solution)/shard_map/all_to_all | solution.py:51
  33.5 0.0 all-reduce.2.cloned.1.call-start
  33.5 53.6 %all-to-all-done = bf16[2,2,4,8,3,1,73,24]{6,7,4,2,1,5,0,3:T(8,128)(2,1)S(1)} async-done(((bf16[2,2,4,8,3,1,73,24]{6,7,4,2,1,5,0,3:T(8,128)(2,1)}), bf16[2,2,4,8,3,1,73,24]{6,7,4,2,1,5,0,3:T(8,128)(2,1)S(1)}, u32[]{:S(2)}, u32[]{:S(2)}) %all-to-all-start) | async-done | bytes 1345568 | tf_op jit(solution)/shard_map/all_to_all | solution.py:51
  87.1 2.1 %copy.33 = bf16[2,2,4,1,3,1,73,8,24]{6,8,7,4,2,1,0,5,3:T(8,128)(2,1)} copy(bf16[2,2,4,1,3,1,73,8,24]{6,8,4,2,1,0,7,5,3:T(8,128)(2,1)S(1)} %bitcast.32) | data formatting | bytes 2691072 | tf_op jit(solution)/shard_map/all_to_all | solution.py:51
  89.2 0.0 all-gather.3.cloned.1.call-done
  89.2 5.1 %multiply_reduce_fusion = f32[12,2,73,720]{3,2,1,0:T(8,128)S(1)} fusion(bf16[192,12,720]{2,0,1:T(8,128)(2,1)} %all-gather.3.cloned.1.call-done, bf16[2,2,12,73,192]{3,4,2,1,0:T(8,128)(2,1)} %bitcast.33), kind=kOutput, calls=%fused_computation | convolution fusion | flops 972570240 | bytes 9709056 | tf_op jit(solution)/shard_map/fpmbcn,nml->fpmbcl/dot_general | solution.py:25
  94.3 0.6 multiply_reduce_fusion.1
  94.9 1.1 copy.56
  96.0 0.0 all-reduce.2.cloned.1.call-update
  96.1 0.0 all-gather.5.cloned.1.call-start
  96.1 71.4 %all-reduce.2.cloned.1.call-done = f32[1,2,73,720]{3,1,2,0:T(2,128)} async-done(((f32[1,2,73,720]{3,1,2,0:T(2,128)}), f32[1,2,73,720]{3,1,2,0:T(2,128)}) %all-reduce.2.cloned.1.call-update) | async-done | bytes 420496 | tf_op jit(solution)/shard_map/psum | solution.py:62
  167.5 0.0 all-gather.5.cloned.1.call-update
  167.6 21.8 %all-gather.5.cloned.1.call-done = f32[4,2,73,720]{3,1,2,0:T(2,128)} async-done(((f32[1,2,73,720]{3,1,2,0:T(2,128)}), f32[4,2,73,720]{3,1,2,0:T(2,128)}) %all-gather.5.cloned.1.call-update) | async-done | bytes 1681936 | tf_op jit(solution)/shard_map/all_gather | solution.py:9
  189.4 2.4 %reduce_sum.38 = f32[2,73,720]{2,0,1:T(2,128)S(1)} reduce(f32[4,2,73,720]{3,1,2,0:T(2,128)} %all-gather.5.cloned.1.call-done, f32[]{:T(128)} %constant.47.clone.1), dimensions={0}, to_apply=%region_3.4 | reduce | flops 315360 | bytes 2102404 | tf_op jit(solution)/shard_map/reduce_sum | solution.py:10
  191.8 1.2 add_log_fusion
  193.0 0.6 fusion.20
  193.6 0.5 broadcast_multiply_fusion.1
  (1 shorter events, 0.0 us)
Async XLA Ops:
  7.2 82.1 %all-gather.3.cloned.1.call-start = ((), (), s32[]{:S(2)}) async-start(), calls=%async_computation.1 | async-start | bytes 4423680 | tf_op jit(solution)/shard_map/all_gather | solution.py:55
  10.5 0.7 copy-start
  10.5 0.8 copy-start.1
  25.9 61.2 %all-to-all-start = ((bf16[2,2,4,8,3,1,73,24]{6,7,4,2,1,5,0,3:T(8,128)(2,1)}), bf16[2,2,4,8,3,1,73,24]{6,7,4,2,1,5,0,3:T(8,128)(2,1)S(1)}, u32[]{:S(2)}, u32[]{:S(2)}) async-start(bf16[2,2,4,8,3,1,73,24]{6,7,4,2,1,5,0,3:T(8,128)(2,1)} %copy.32), calls=%async_computation | async-start | bytes 4718592 | tf_op jit(solution)/shard_map/all_to_all | solution.py:51
  33.5 134.1 %all-reduce.2.cloned.1.call-start = ((), (), s32[]{:S(2)}) async-start(), calls=%async_computation.2 | async-start | bytes 897024 | tf_op jit(solution)/shard_map/psum | solution.py:62
  96.1 93.3 %all-gather.5.cloned.1.call-start = ((), (), s32[]{:S(2)}) async-start(), calls=%async_computation.3 | async-start | bytes 2242560 | tf_op jit(solution)/shard_map/all_gather | solution.py:9
Sparse Core Ops, SparseCore 0:
  9.5 33.4 all-gather.2
  96.2 71.2 all-reduce.1
  169.1 20.2 all-gather.4
